TPU v7x, 32 devices: a whole 2x2x4 slice. The times are simulated.
32 devices in a mesh: gx: 2 (over core), gy: 4 (over y, x), gz: 4 (over z).
Axes of the slice: x: 2, y: 2, z: 4, core: 2. Of those that a mesh axis runs over, the one named last changes fastest.
Arguments:
- block_values: bfloat16 [4, 64, 4, 6, 128, 128], P('gy', 'gx', 'gz'), as said below
- block_cols: int32 [4, 64, 4, 6], P('gy', 'gx', 'gz'), may hold values from 0 to 63, as said below
Outputs:
- purified: float32 [256, 32768], P(('gx', 'gy'), 'gz')
Inputs may be any that keep to these rules, and one draw needn't show every extreme that they name: block_cols[a, s, b, :] holds 6 distinct tile columns of panel b at which tile row a * 64 + s of P is nonzero; every tile column of a panel is listed by exactly 6 tile rows of each slab; the pattern is symmetric: tile (i, j) is listed exactly when tile (j, i) is. `block_values`: P is symmetric: the tile listed at (i, j) is the transpose of the tile listed at (j, i), and diagonal tiles are symmetric.
All inputs are finite; a program needn't handle non-finite values.
Results may differ from a plain program's by a relative error of at most 0.0033.
Values may be sent and summed in bfloat16 or wider, within the bound.
No kernel may reach another device: no remote copies, remote signals or barrier semaphores. Data moves between devices by JAX's collectives and lax.ppermute only.
A program may use at most 128 MiB of HBM per device.

v0:
```python
import functools

import jax
import jax.numpy as jnp
from jax import lax
from jax.experimental import pallas as pl
from jax.experimental.pallas import tpu as pltpu
from jax.sharding import PartitionSpec as P

WIN = 1
UNROLL = 4
VMEM = pltpu.MemorySpace.VMEM
SMEM = pltpu.MemorySpace.SMEM


def limit(mib):
    return pltpu.CompilerParams(vmem_limit_bytes=mib << 20)


def assemble_kernel(parts, *refs):
    part_refs, out_ref, sems = refs[:parts], refs[parts], refs[parts + 1]
    here = part_refs[0].shape[0]
    copies = [
        pltpu.make_async_copy(part_refs[t], out_ref.at[pl.ds(t * here, here)], sems.at[t])
        for t in range(parts)
    ]
    for copy in copies:
        copy.start()
    for copy in copies:
        copy.wait()


def assemble(parts):
    here = parts[0].shape[0]
    shape = (here * len(parts),) + parts[0].shape[1:]
    return pl.pallas_call(
        functools.partial(assemble_kernel, len(parts)),
        out_shape=pltpu.VMEM(shape, jnp.bfloat16),
        in_specs=[pl.BlockSpec(memory_space=pltpu.HBM)] * len(parts),
        out_specs=pl.BlockSpec(memory_space=VMEM),
        scratch_shapes=[pltpu.SemaphoreType.DMA((len(parts),))],
        compiler_params=limit(50),
        cost_estimate=pl.CostEstimate(flops=4_000_000, bytes_accessed=25_000_000, transcendentals=0),
        name="assemble",
    )(*parts)


def swaps(size, step):
    return [(i, i ^ step) for i in range(size)]


def invert_kernel(cols_ref, inv_ref, count_ref):
    rows, slots = cols_ref.shape

    @pl.loop(0, rows)
    def _(y):
        count_ref[y] = 0

    @pl.loop(0, rows)
    def _(p):
        ys = [cols_ref[p, j] for j in range(slots)]
        ns = [count_ref[y] for y in ys]
        for j in range(slots):
            inv_ref[ys[j], ns[j]] = p * 8 + j
        for j in range(slots):
            count_ref[ys[j]] = ns[j] + 1


def invert(columns):
    return pl.pallas_call(
        invert_kernel,
        out_shape=jax.ShapeDtypeStruct(columns.shape, jnp.int32),
        in_specs=[pl.BlockSpec(memory_space=SMEM)],
        out_specs=pl.BlockSpec(memory_space=SMEM),
        scratch_shapes=[pltpu.SMEM((columns.shape[0],), jnp.int32)],
        compiler_params=limit(1),
        cost_estimate=pl.CostEstimate(flops=4_000_000, bytes_accessed=4096, transcendentals=0),
        name="invert",
    )(columns)


def product_one_kernel(by_rows, here, lefts, index_ref, slab_ref, *refs):
    left_refs, refs = refs[:lefts], refs[lefts:]
    blocks = len(refs) - 2
    send_refs, (left_ref, acc_ref) = refs[:blocks], refs[blocks:]
    g, a, b = lax.axis_index("gx"), lax.axis_index("gy"), lax.axis_index("gz")
    slab, slots = slab_ref.shape[:2]
    rows = acc_ref.shape[2]
    height = blocks * rows
    chosen = a ^ b if by_rows else a
    for k in range(lefts):

        @pl.when(chosen == k)
        def _(k=k):
            left_ref[...] = left_refs[k][...]

    tail = left_ref[pl.ds(slots * height, 16), :].astype(jnp.float32)
    columns = [jnp.max(tail[k : k + 1, :]).astype(jnp.int32) for k in range(slots)]
    acc_ref[...] = jnp.zeros_like(acc_ref)
    for k in range(slots):
        left = left_ref[pl.ds(k * height, height), :]
        if by_rows:
            p = lax.rem(columns[k] + slab - here * g, slab)
            targets = [index_ref[p, j] for j in range(slots)]
            tiles = [slab_ref[p, j] for j in range(slots)]
        else:
            entries = [index_ref[columns[k], n] for n in range(slots)]
            targets = [entry >> 3 for entry in entries]
            tiles = [slab_ref[entry >> 3, entry & 7] for entry in entries]
        products = [
            lax.dot_general(
                left,
                tile,
                (((1,), (0 if by_rows else 1,)), ((), ())),
                preferred_element_type=jnp.float32,
            )
            for tile in tiles
        ]
        for n in range(slots):
            for q in range(blocks):
                acc_ref[q, targets[n]] += products[n][q * rows : (q + 1) * rows]
    me = a if by_rows else b
    for k in range(blocks):
        send_refs[k][...] = acc_ref[me ^ k].astype(jnp.bfloat16)


def product_one(by_rows, index, lefts, tiles, here, blocks, height):
    slab, _ = index.shape
    tile = tiles.shape[2]
    rows = height // blocks
    message = jax.ShapeDtypeStruct((slab, rows, tile), jnp.bfloat16)
    return pl.pallas_call(
        functools.partial(product_one_kernel, by_rows, here, len(lefts)),
        out_shape=[message] * blocks,
        in_specs=[pl.BlockSpec(memory_space=SMEM)]
        + [pl.BlockSpec(memory_space=VMEM)] * (1 + len(lefts)),
        out_specs=[pl.BlockSpec(memory_space=VMEM)] * blocks,
        scratch_shapes=[
            pltpu.VMEM(lefts[0].shape, jnp.bfloat16),
            pltpu.VMEM((blocks, slab, rows, tile), jnp.float32),
        ],
        compiler_params=limit(20),
        cost_estimate=pl.CostEstimate(flops=12_000_000, bytes_accessed=4_000_000, transcendentals=0),
        name="one_rows" if by_rows else "one_columns",
    )(index, tiles, *lefts)


def product_two_kernel(by_rows, here, blocks, index_ref, slab_ref, *refs):
    round_refs, refs = refs[:blocks], refs[blocks:]
    send_refs, (left_ref,) = refs[:blocks], refs[blocks:]
    g, a, b = lax.axis_index("gx"), lax.axis_index("gy"), lax.axis_index("gz")
    slab, slots = slab_ref.shape[:2]
    rows = left_ref.shape[2]
    for k in range(blocks):
        left_ref[a ^ b ^ k] = round_refs[k][...]
    extra = jnp.where(a == b, 3.0, 0.0).astype(jnp.float32)

    def left_of(p):
        return jnp.concatenate([left_ref[m, p] for m in range(blocks)], axis=0)

    def one(q, lefts, tiles, same):
        summed = None
        for n in range(0, slots, 2):
            left = jnp.concatenate([left_of(p) for p in lefts[n : n + 2]], axis=1)
            pair = jnp.concatenate(tiles[n : n + 2], axis=1 if by_rows else 0)
            product = lax.dot_general(
                left,
                pair,
                (((1,), (1 if by_rows else 0,)), ((), ())),
                preferred_element_type=jnp.float32,
            )
            summed = product if summed is None else summed + product
        for m in range(blocks):
            value = extra * left_ref[m, same].astype(jnp.float32) - 2.0 * summed[m * rows : (m + 1) * rows]
            send_refs[m][q] = value.astype(jnp.bfloat16)

    @pl.loop(0, slab, step=UNROLL)
    def _(first):
        for u in range(UNROLL):
            q = first + u
            entries = [index_ref[q, n] for n in range(slots)]
            if by_rows:
                tiles = [slab_ref[q, j] for j in range(slots)]
                one(q, entries, tiles, lax.rem(q + here * g, slab))
            else:
                lefts = [entry >> 3 for entry in entries]
                tiles = [slab_ref[entry >> 3, entry & 7] for entry in entries]
                one(q, lefts, tiles, lax.rem(q + slab - here * g, slab))


def product_two(by_rows, index, rounded, tiles, here):
    slab, _ = index.shape
    blocks = len(rounded)
    tile = tiles.shape[2]
    rows = rounded[0].shape[1]
    message = jax.ShapeDtypeStruct((slab, rows, tile), jnp.bfloat16)
    return pl.pallas_call(
        functools.partial(product_two_kernel, by_rows, here, blocks),
        out_shape=[message] * blocks,
        in_specs=[pl.BlockSpec(memory_space=SMEM)]
        + [pl.BlockSpec(memory_space=VMEM)] * (1 + blocks),
        out_specs=[pl.BlockSpec(memory_space=VMEM)] * blocks,
        scratch_shapes=[pltpu.VMEM((blocks, slab, rows, tile), jnp.bfloat16)],
        compiler_params=limit(20),
        cost_estimate=pl.CostEstimate(flops=30_000_000, bytes_accessed=12_000_000, transcendentals=0),
        name="two_rows" if by_rows else "two_columns",
    )(index, tiles, *rounded)


def finish_kernel(here, *refs):
    half = len(refs) // 2
    first, second, out_ref = refs[:half], refs[half:-1], refs[-1]
    g = lax.axis_index("gx")
    slab, rows, tile = first[0].shape

    def add(refs_in, y):
        total = refs_in[0][y].astype(jnp.float32)
        for ref in refs_in[1:]:
            total = total + ref[y].astype(jnp.float32)
        return total

    @pl.loop(0, slab, unroll=8)
    def _(y):
        columns = pl.ds(pl.multiple_of(y * tile, tile), tile)
        out_ref[0:rows, columns] = add(first, y)
        out_ref[rows : 2 * rows, columns] = add(second, lax.rem(y + slab - here * g, slab))


def finish(first, second, here):
    slab, rows, tile = first[0].shape
    return pl.pallas_call(
        functools.partial(finish_kernel, here),
        out_shape=jax.ShapeDtypeStruct((2 * rows, slab * tile), jnp.float32),
        in_specs=[pl.BlockSpec(memory_space=VMEM)] * (len(first) + len(second)),
        out_specs=pl.BlockSpec(memory_space=VMEM),
        compiler_params=limit(8),
        name="finish",
    )(*first, *second)


def total(values):
    summed = values[0].astype(jnp.float32)
    for value in values[1:]:
        summed = summed + value.astype(jnp.float32)
    return summed.astype(jnp.bfloat16)


def local(block_values, block_cols):
    tiles_here = block_values[0, :, 0]
    columns_here = block_cols[0, :, 0]
    here, slots, tile, _ = tiles_here.shape
    parts = lax.axis_size("gx")
    size = lax.axis_size("gy")
    blocks = WIN * tile // size
    rows = blocks // 2
    height = rows * size

    def payload(first):
        window = tiles_here[0].reshape(slots, size, blocks, tile)[:, :, first : first + rows]
        tail = jnp.broadcast_to(columns_here[0].astype(jnp.bfloat16)[:, None], (slots, tile))
        tail = jnp.pad(tail, ((0, 16 - slots), (0, 0)))
        return jnp.concatenate([window.reshape(slots * height, tile), tail], axis=0)

    pay_a, pay_b = payload(0), payload(rows)
    both = ("gy", "gz")
    shifts = [[((i + t) % parts, i) for i in range(parts)] for t in range(1, parts)]
    left_a = [pay_a] + [lax.ppermute(pay_a, "gy", [(0, k)]) for k in range(1, size)]
    columns = jnp.concatenate([columns_here] + [lax.ppermute(columns_here, "gx", s) for s in shifts], axis=0)
    inverse = invert(columns)
    moved = [lax.ppermute(tiles_here, "gx", s) for s in shifts]
    left_b = [
        lax.ppermute(pay_b, both, [(a, a * size + (a ^ k)) for a in range(size)]) for k in range(size)
    ]
    tiles = assemble([tiles_here] + moved)

    def scatter(sends, axis):
        return [sends[0]] + [lax.ppermute(sends[k], axis, swaps(size, k)) for k in range(1, size)]

    def spread(own, axis):
        return [own] + [lax.ppermute(own, axis, swaps(size, k)) for k in range(1, size)]

    sends_a = product_one(False, inverse, left_a, tiles, here, size, height)
    parts_a = scatter(sends_a, "gz")
    _, left_b = lax.optimization_barrier((sends_a[0], left_b))
    sends_b = product_one(True, columns, left_b, tiles, here, size, height)
    parts_b = scatter(sends_b, "gy")
    own_b = total(parts_b)
    own_a = total(parts_a)
    rounded_b = spread(own_b, "gy")
    rounded_a = spread(own_a, "gz")
    out_b = product_two(True, columns, rounded_b, tiles, here)
    got_b = [
        lax.ppermute(
            out_b[m],
            both,
            [(a * size + b, (b ^ m) * size + a) for a in range(size) for b in range(size)],
        )
        for m in range(size)
    ]
    out_a = product_two(False, inverse, rounded_a, tiles, here)
    got_a = scatter(out_a, "gy")
    return finish(got_a, got_b, here)


def solution(mesh):
    in_specs = (P("gy", "gx", "gz", None, None, None), P("gy", "gx", "gz", None))
    out_specs = P(("gx", "gy"), "gz")
    return jax.shard_map(local, mesh=mesh, in_specs=in_specs, out_specs=out_specs, check_vma=False)
```

profile of v0, /device:TPU:4, one launch (start us, length us, event | category | flops | bytes accessed | tf_op | source)
XLA Modules:
  0.0 171.0 jit_solution(8539075937668088843)
XLA Ops:
  0.0 0.7 copy.10
  0.7 0.5 collective-permute-start
  1.2 0.9 slice.17
  2.1 0.8 fusion
  3.0 0.1 pad_maximum_fusion.1
  3.1 0.7 collective-permute-start.2
  3.8 1.3 collective-permute-start.3
  5.1 0.7 collective-permute-start.4
  5.8 4.7 %collective-permute-done = s32[32,6]{0,1:T(8,128)S(1)} collective-permute-done((s32[32,6]{0,1:T(8,128)S(1)}, s32[32,6]{0,1:T(8,128)S(1)}, u32[]{:S(2)}, u32[]{:S(2)}) %collective-permute-start) | collective-permute-done | bytes 800 | tf_op jit(solution)/shard_map/ppermute | solution.py:268
  10.5 0.1 pad_add_fusion
  10.6 0.1 copy.5.cols_ref.index_ref
  10.7 4.3 %invert.1.index_ref = s32[64,6]{1,0:T(8,128)S(1)} custom-call(s32[64,6]{1,0:T(8,128)S(1)} %copy.5.cols_ref.index_ref), custom_call_target="tpu_custom_call" | custom-call | flops 4000000 | bytes 4096 | tf_op jit(solution)/shard_map/invert/pallas_call | solution.py:70
  15.0 4.6 %assemble.1.slab_ref = bf16[64,6,128,128]{3,2,1,0:T(8,128)(2,1)S(1)} custom-call(bf16[32,6,128,128]{3,2,1,0:T(8,128)(2,1)} %bitcast.8, bf16[32,6,128,128]{3,2,1,0:T(8,128)(2,1)} %collective-permute-done.1.refs_1_), custom_call_target="tpu_custom_call" | custom-call | flops 4000000 | bytes 25000000 | tf_op jit(solution)/shard_map/assemble/pallas_call | solution.py:36
  19.6 0.0 collective-permute-done.2.refs_1_
  19.6 0.0 collective-permute-done.3.refs_2_
  19.7 2.3 %one_columns.1 = (bf16[64,16,128]{2,1,0:T(8,128)(2,1)S(1)}, bf16[64,16,128]{2,1,0:T(8,128)(2,1)S(1)}, bf16[64,16,128]{2,1,0:T(8,128)(2,1)S(1)}, bf16[64,16,128]{2,1,0:T(8,128)(2,1)S(1)}) custom-call(s32[64,6]{1,0:T(8,128)S(1)} %invert.1.index_ref, bf16[64,6,128,128]{3,2,1,0:T(8,128)(2,1)S(1)} %assemble.1.slab_ref, ...), custom_call_target="tpu_custom_call" | custom-call | flops 12000000 | bytes 4000000 | tf_op jit(solution)/shard_map/one_columns/pallas_call | solution.py:132
  22.0 3.7 %collective-permute-start.7 = (bf16[64,16,128]{2,1,0:T(8,128)(2,1)S(1)}, bf16[64,16,128]{2,1,0:T(8,128)(2,1)S(1)}, u32[]{:S(2)}, u32[]{:S(2)}) collective-permute-start(bf16[64,16,128]{2,1,0:T(8,128)(2,1)S(1)} %get-tuple-element.28), channel_id=1, source_target_pairs={{0,3},{1,2},{2,1},{3,0},{4,7},{5,6},{6,5},{7,4},{8,11},{9,10},{10,... | collective-permute-start | bytes 786440 | tf_op jit(solution)/shard_map/ppermute | solution.py:277
  25.6 0.8 collective-permute-start.5
  26.4 0.7 collective-permute-start.14
  27.1 0.7 collective-permute-start.15
  27.8 1.3 collective-permute-start.16
  29.1 0.7 collective-permute-start.17
  29.8 25.9 %collective-permute-done.16.refs_2_ = bf16[400,128]{1,0:T(8,128)(2,1)S(1)} collective-permute-done((bf16[400,128]{1,0:T(8,128)(2,1)S(1)}, bf16[400,128]{1,0:T(8,128)(2,1)S(1)}, u32[]{:S(2)}, u32[]{:S(2)}) %collective-permute-start.16) | collective-permute-done | bytes 102432 | tf_op jit(solution)/shard_map/ppermute | solution.py:272
  55.6 1.8 %one_rows.1 = (bf16[64,16,128]{2,1,0:T(8,128)(2,1)S(1)}, bf16[64,16,128]{2,1,0:T(8,128)(2,1)S(1)}, bf16[64,16,128]{2,1,0:T(8,128)(2,1)S(1)}, bf16[64,16,128]{2,1,0:T(8,128)(2,1)S(1)}) custom-call(s32[64,6]{1,0:T(8,128)S(1)} %copy.5.cols_ref.index_ref, bf16[64,6,128,128]{3,2,1,0:T(8,128)(2,1)S(1)} %assemble.1.slab_ref, ...), custom_call_target="tpu_custom_call" | custom-call | flops 12000000 | bytes 4000000 | tf_op jit(solution)/shard_map/one_rows/pallas_call | solution.py:132
  57.5 0.1 collective-permute-start.20
  57.5 0.1 collective-permute-start.19
  57.6 3.4 %collective-permute-start.18 = (bf16[64,16,128]{2,1,0:T(8,128)(2,1)S(1)}, bf16[64,16,128]{2,1,0:T(8,128)(2,1)S(1)}, u32[]{:S(2)}, u32[]{:S(2)}) collective-permute-start(bf16[64,16,128]{2,1,0:T(8,128)(2,1)S(1)} %get-tuple-element.38), channel_id=1, source_target_pairs={{0,4},{4,0},{8,12},{12,8},{1,5},{5,1},{9,13},{13,9},{2,6},{6,2},{1... | collective-permute-start | bytes 786440 | tf_op jit(solution)/shard_map/ppermute | solution.py:277
  61.0 0.2 add_convert_fusion.1.refs_0_
  61.2 2.0 %collective-permute-start.8 = (bf16[64,16,128]{2,1,0:T(8,128)(2,1)S(1)}, bf16[64,16,128]{2,1,0:T(8,128)(2,1)S(1)}, u32[]{:S(2)}, u32[]{:S(2)}) collective-permute-start(bf16[64,16,128]{2,1,0:T(8,128)(2,1)S(1)} %add_convert_fusion.1.refs_0_), channel_id=1, source_target_pairs={{0,1},{1,0},{2,3},{3,2},{4,5},{5,4},{6,7},{7,6},{8,9},{9,8},{10,11... | collective-permute-start | bytes 786440 | tf_op jit(solution)/shard_map/ppermute | solution.py:280
  63.2 4.4 %collective-permute-done.20 = bf16[64,16,128]{2,1,0:T(8,128)(2,1)S(1)} collective-permute-done((bf16[64,16,128]{2,1,0:T(8,128)(2,1)S(1)}, bf16[64,16,128]{2,1,0:T(8,128)(2,1)S(1)}, u32[]{:S(2)}, u32[]{:S(2)}) %collective-permute-start.20) | collective-permute-done | bytes 262176 | tf_op jit(solution)/shard_map/ppermute | solution.py:277
  67.6 1.1 collective-permute-start.10
  68.7 1.2 collective-permute-done.19
  69.9 0.2 add_convert_fusion.refs_0_
  70.0 0.3 collective-permute-start.21
  70.4 2.0 %collective-permute-start.22 = (bf16[64,16,128]{2,1,0:T(8,128)(2,1)S(1)}, bf16[64,16,128]{2,1,0:T(8,128)(2,1)S(1)}, u32[]{:S(2)}, u32[]{:S(2)}) collective-permute-start(bf16[64,16,128]{2,1,0:T(8,128)(2,1)S(1)} %add_convert_fusion.refs_0_), channel_id=1, source_target_pairs={{0,8},{4,12},{8,0},{12,4},{1,9},{5,13},{9,1},{13,5},{2,10},{6,14},... | collective-permute-start | bytes 786440 | tf_op jit(solution)/shard_map/ppermute | solution.py:280
  72.3 1.3 collective-permute-start.23
  73.6 10.5 %collective-permute-done.9.refs_2_ = bf16[64,16,128]{2,1,0:T(8,128)(2,1)S(1)} collective-permute-done((bf16[64,16,128]{2,1,0:T(8,128)(2,1)S(1)}, bf16[64,16,128]{2,1,0:T(8,128)(2,1)S(1)}, u32[]{:S(2)}, u32[]{:S(2)}) %collective-permute-start.9) | collective-permute-done | bytes 262176 | tf_op jit(solution)/shard_map/ppermute | solution.py:280
  84.1 5.7 %two_columns.1 = (bf16[64,16,128]{2,1,0:T(8,128)(2,1)S(1)}, bf16[64,16,128]{2,1,0:T(8,128)(2,1)S(1)}, bf16[64,16,128]{2,1,0:T(8,128)(2,1)S(1)}, bf16[64,16,128]{2,1,0:T(8,128)(2,1)S(1)}) custom-call(s32[64,6]{1,0:T(8,128)S(1)} %invert.1.index_ref, bf16[64,6,128,128]{3,2,1,0:T(8,128)(2,1)S(1)} %assemble.1.slab_ref, ...), custom_call_target="tpu_custom_call" | custom-call | flops 30000000 | bytes 12000000 | tf_op jit(solution)/shard_map/two_columns/pallas_call | solution.py:197
  89.8 0.5 collective-permute-start.11
  90.3 0.1 collective-permute-start.12
  90.3 3.0 %collective-permute-start.13 = (bf16[64,16,128]{2,1,0:T(8,128)(2,1)S(1)}, bf16[64,16,128]{2,1,0:T(8,128)(2,1)S(1)}, u32[]{:S(2)}, u32[]{:S(2)}) collective-permute-start(bf16[64,16,128]{2,1,0:T(8,128)(2,1)S(1)} %get-tuple-element.32), channel_id=1, source_target_pairs={{0,12},{4,8},{8,4},{12,0},{1,13},{5,9},{9,5},{13,1},{2,14},{6,10},... | collective-permute-start | bytes 786440 | tf_op jit(solution)/shard_map/ppermute | solution.py:277
  93.4 7.5 %two_rows.1 = (bf16[64,16,128]{2,1,0:T(8,128)(2,1)S(1)}, bf16[64,16,128]{2,1,0:T(8,128)(2,1)S(1)}, bf16[64,16,128]{2,1,0:T(8,128)(2,1)S(1)}, bf16[64,16,128]{2,1,0:T(8,128)(2,1)S(1)}) custom-call(s32[64,6]{1,0:T(8,128)S(1)} %copy.5.cols_ref.index_ref, bf16[64,6,128,128]{3,2,1,0:T(8,128)(2,1)S(1)} %assemble.1.slab_ref, ...), custom_call_target="tpu_custom_call" | custom-call | flops 30000000 | bytes 12000000 | tf_op jit(solution)/shard_map/two_rows/pallas_call | solution.py:197
  100.8 6.4 %collective-permute-start.24 = (bf16[64,16,128]{2,1,0:T(8,128)(2,1)S(1)}, bf16[64,16,128]{2,1,0:T(8,128)(2,1)S(1)}, u32[]{:S(2)}, u32[]{:S(2)}) collective-permute-start(bf16[64,16,128]{2,1,0:T(8,128)(2,1)S(1)} %get-tuple-element.41), channel_id=1, source_target_pairs={{0,0},{1,4},{2,8},{3,12},{4,1},{5,5},{6,9},{7,13},{8,2},{9,6},{10,... | collective-permute-start | bytes 786440 | tf_op jit(solution)/shard_map/ppermute | solution.py:293
  107.2 2.6 %collective-permute-start.25 = (bf16[64,16,128]{2,1,0:T(8,128)(2,1)S(1)}, bf16[64,16,128]{2,1,0:T(8,128)(2,1)S(1)}, u32[]{:S(2)}, u32[]{:S(2)}) collective-permute-start(bf16[64,16,128]{2,1,0:T(8,128)(2,1)S(1)} %get-tuple-element.42), channel_id=1, source_target_pairs={{0,4},{1,0},{2,12},{3,8},{4,5},{5,1},{6,13},{7,9},{8,6},{9,2},{10,... | collective-permute-start | bytes 786440 | tf_op jit(solution)/shard_map/ppermute | solution.py:293
  109.8 3.6 %collective-permute-start.27 = (bf16[64,16,128]{2,1,0:T(8,128)(2,1)S(1)}, bf16[64,16,128]{2,1,0:T(8,128)(2,1)S(1)}, u32[]{:S(2)}, u32[]{:S(2)}) collective-permute-start(bf16[64,16,128]{2,1,0:T(8,128)(2,1)S(1)} %get-tuple-element.44), channel_id=1, source_target_pairs={{0,12},{1,8},{2,4},{3,0},{4,13},{5,9},{6,5},{7,1},{8,14},{9,10},{1... | collective-permute-start | bytes 786440 | tf_op jit(solution)/shard_map/ppermute | solution.py:293
  113.5 20.7 %collective-permute-done.24.refs_4_ = bf16[64,16,128]{2,1,0:T(8,128)(2,1)S(1)} collective-permute-done((bf16[64,16,128]{2,1,0:T(8,128)(2,1)S(1)}, bf16[64,16,128]{2,1,0:T(8,128)(2,1)S(1)}, u32[]{:S(2)}, u32[]{:S(2)}) %collective-permute-start.24) | collective-permute-done | bytes 262176 | tf_op jit(solution)/shard_map/ppermute | solution.py:293
  134.2 35.4 %collective-permute-done.27.refs_7_ = bf16[64,16,128]{2,1,0:T(8,128)(2,1)S(1)} collective-permute-done((bf16[64,16,128]{2,1,0:T(8,128)(2,1)S(1)}, bf16[64,16,128]{2,1,0:T(8,128)(2,1)S(1)}, u32[]{:S(2)}, u32[]{:S(2)}) %collective-permute-start.27) | collective-permute-done | bytes 262176 | tf_op jit(solution)/shard_map/ppermute | solution.py:293
  169.6 1.4 finish.1
  (25 shorter events, 0.1 us)
Async XLA Ops:
  0.0 15.0 %collective-permute-start.1 = (bf16[32,6,128,128]{3,2,1,0:T(8,128)(2,1)}, bf16[32,6,128,128]{3,2,1,0:T(8,128)(2,1)}, u32[]{:S(2)}, u32[]{:S(2)}) collective-permute-start(bf16[32,6,128,128]{3,2,1,0:T(8,128)(2,1)} %bitcast.7), channel_id=1, source_target_pairs={{16,0},{0,16},{17,1},{1,17},{18,2},{2,18},{19,3},{3,19},{20,4},{4,... | collective-permute-start | bytes 18874376 | tf_op jit(solution)/shard_map/ppermute | solution.py:270
  0.7 9.8 %collective-permute-start = (s32[32,6]{0,1:T(8,128)S(1)}, s32[32,6]{0,1:T(8,128)S(1)}, u32[]{:S(2)}, u32[]{:S(2)}) collective-permute-start(s32[32,6]{0,1:T(8,128)S(1)} %bitcast.12), channel_id=1, source_target_pairs={{16,0},{0,16},{17,1},{1,17},{18,2},{2,18},{19,3},{3,19},{20,4},{4,... | collective-permute-start | bytes 2312 | tf_op jit(solution)/shard_map/ppermute | solution.py:268
  3.1 16.5 %collective-permute-start.2 = (bf16[400,128]{1,0:T(8,128)(2,1)S(1)}, bf16[400,128]{1,0:T(8,128)(2,1)S(1)}, u32[]{:S(2)}, u32[]{:S(2)}) collective-permute-start(bf16[400,128]{1,0:T(8,128)(2,1)S(1)} %get-tuple-element.48.refs_0_), channel_id=1, source_target_pairs={{0,4},{1,5},{2,6},{3,7},{16,20},{17,21},{18,22},{19,23}} | collective-permute-start | bytes 307208 | tf_op jit(solution)/shard_map/ppermute | solution.py:267
  3.8 15.9 %collective-permute-start.3 = (bf16[400,128]{1,0:T(8,128)(2,1)S(1)}, bf16[400,128]{1,0:T(8,128)(2,1)S(1)}, u32[]{:S(2)}, u32[]{:S(2)}) collective-permute-start(bf16[400,128]{1,0:T(8,128)(2,1)S(1)} %get-tuple-element.48.refs_0_), channel_id=1, source_target_pairs={{0,8},{1,9},{2,10},{3,11},{16,24},{17,25},{18,26},{19,27}} | collective-permute-start | bytes 307208 | tf_op jit(solution)/shard_map/ppermute | solution.py:267
  5.1 14.6 %collective-permute-start.4 = (bf16[400,128]{1,0:T(8,128)(2,1)S(1)}, bf16[400,128]{1,0:T(8,128)(2,1)S(1)}, u32[]{:S(2)}, u32[]{:S(2)}) collective-permute-start(bf16[400,128]{1,0:T(8,128)(2,1)S(1)} %get-tuple-element.48.refs_0_), channel_id=1, source_target_pairs={{0,12},{1,13},{2,14},{3,15},{16,28},{17,29},{18,30},{19,31}} | collective-permute-start | bytes 307208 | tf_op jit(solution)/shard_map/ppermute | solution.py:267
  22.0 35.7 %collective-permute-start.7 = (bf16[64,16,128]{2,1,0:T(8,128)(2,1)S(1)}, bf16[64,16,128]{2,1,0:T(8,128)(2,1)S(1)}, u32[]{:S(2)}, u32[]{:S(2)}) collective-permute-start(bf16[64,16,128]{2,1,0:T(8,128)(2,1)S(1)} %get-tuple-element.28), channel_id=1, source_target_pairs={{0,3},{1,2},{2,1},{3,0},{4,7},{5,6},{6,5},{7,4},{8,11},{9,10},{10,... | collective-permute-start | bytes 786440 | tf_op jit(solution)/shard_map/ppermute | solution.py:277
  25.6 35.4 %collective-permute-start.6 = (bf16[64,16,128]{2,1,0:T(8,128)(2,1)S(1)}, bf16[64,16,128]{2,1,0:T(8,128)(2,1)S(1)}, u32[]{:S(2)}, u32[]{:S(2)}) collective-permute-start(bf16[64,16,128]{2,1,0:T(8,128)(2,1)S(1)} %get-tuple-element.27), channel_id=1, source_target_pairs={{0,2},{1,3},{2,0},{3,1},{4,6},{5,7},{6,4},{7,5},{8,10},{9,11},{10,... | collective-permute-start | bytes 786440 | tf_op jit(solution)/shard_map/ppermute | solution.py:277
  25.6 35.4 %collective-permute-start.5 = (bf16[64,16,128]{2,1,0:T(8,128)(2,1)S(1)}, bf16[64,16,128]{2,1,0:T(8,128)(2,1)S(1)}, u32[]{:S(2)}, u32[]{:S(2)}) collective-permute-start(bf16[64,16,128]{2,1,0:T(8,128)(2,1)S(1)} %get-tuple-element.26), channel_id=1, source_target_pairs={{0,1},{1,0},{2,3},{3,2},{4,5},{5,4},{6,7},{7,6},{8,9},{9,8},{10,11... | collective-permute-start | bytes 786440 | tf_op jit(solution)/shard_map/ppermute | solution.py:277
  26.4 1.3 collective-permute-start.14
  27.1 2.0 %collective-permute-start.15 = (bf16[400,128]{1,0:T(8,128)(2,1)S(1)}, bf16[400,128]{1,0:T(8,128)(2,1)S(1)}, u32[]{:S(2)}, u32[]{:S(2)}) collective-permute-start(bf16[400,128]{1,0:T(8,128)(2,1)S(1)} %get-tuple-element.47), channel_id=1, source_target_pairs={{0,1},{1,4},{2,11},{3,14},{16,17},{17,20},{18,27},{19,30}} | collective-permute-start | bytes 307208 | tf_op jit(solution)/shard_map/ppermute | solution.py:272
  27.8 27.8 %collective-permute-start.16 = (bf16[400,128]{1,0:T(8,128)(2,1)S(1)}, bf16[400,128]{1,0:T(8,128)(2,1)S(1)}, u32[]{:S(2)}, u32[]{:S(2)}) collective-permute-start(bf16[400,128]{1,0:T(8,128)(2,1)S(1)} %get-tuple-element.47), channel_id=1, source_target_pairs={{0,2},{1,7},{2,8},{3,13},{16,18},{17,23},{18,24},{19,29}} | collective-permute-start | bytes 307208 | tf_op jit(solution)/shard_map/ppermute | solution.py:272
  29.1 26.5 %collective-permute-start.17 = (bf16[400,128]{1,0:T(8,128)(2,1)S(1)}, bf16[400,128]{1,0:T(8,128)(2,1)S(1)}, u32[]{:S(2)}, u32[]{:S(2)}) collective-permute-start(bf16[400,128]{1,0:T(8,128)(2,1)S(1)} %get-tuple-element.47), channel_id=1, source_target_pairs={{0,3},{1,6},{2,9},{3,12},{16,19},{17,22},{18,25},{19,28}} | collective-permute-start | bytes 307208 | tf_op jit(solution)/shard_map/ppermute | solution.py:272
  57.5 10.1 %collective-permute-start.20 = (bf16[64,16,128]{2,1,0:T(8,128)(2,1)S(1)}, bf16[64,16,128]{2,1,0:T(8,128)(2,1)S(1)}, u32[]{:S(2)}, u32[]{:S(2)}) collective-permute-start(bf16[64,16,128]{2,1,0:T(8,128)(2,1)S(1)} %get-tuple-element.40), channel_id=1, source_target_pairs={{0,12},{4,8},{8,4},{12,0},{1,13},{5,9},{9,5},{13,1},{2,14},{6,10},... | collective-permute-start | bytes 786440 | tf_op jit(solution)/shard_map/ppermute | solution.py:277
  57.5 12.3 %collective-permute-start.19 = (bf16[64,16,128]{2,1,0:T(8,128)(2,1)S(1)}, bf16[64,16,128]{2,1,0:T(8,128)(2,1)S(1)}, u32[]{:S(2)}, u32[]{:S(2)}) collective-permute-start(bf16[64,16,128]{2,1,0:T(8,128)(2,1)S(1)} %get-tuple-element.39), channel_id=1, source_target_pairs={{0,8},{4,12},{8,0},{12,4},{1,9},{5,13},{9,1},{13,5},{2,10},{6,14},... | collective-permute-start | bytes 786440 | tf_op jit(solution)/shard_map/ppermute | solution.py:277
  57.6 12.2 %collective-permute-start.18 = (bf16[64,16,128]{2,1,0:T(8,128)(2,1)S(1)}, bf16[64,16,128]{2,1,0:T(8,128)(2,1)S(1)}, u32[]{:S(2)}, u32[]{:S(2)}) collective-permute-start(bf16[64,16,128]{2,1,0:T(8,128)(2,1)S(1)} %get-tuple-element.38), channel_id=1, source_target_pairs={{0,4},{4,0},{8,12},{12,8},{1,5},{5,1},{9,13},{13,9},{2,6},{6,2},{1... | collective-permute-start | bytes 786440 | tf_op jit(solution)/shard_map/ppermute | solution.py:277
  61.2 11.2 %collective-permute-start.8 = (bf16[64,16,128]{2,1,0:T(8,128)(2,1)S(1)}, bf16[64,16,128]{2,1,0:T(8,128)(2,1)S(1)}, u32[]{:S(2)}, u32[]{:S(2)}) collective-permute-start(bf16[64,16,128]{2,1,0:T(8,128)(2,1)S(1)} %add_convert_fusion.1.refs_0_), channel_id=1, source_target_pairs={{0,1},{1,0},{2,3},{3,2},{4,5},{5,4},{6,7},{7,6},{8,9},{9,8},{10,11... | collective-permute-start | bytes 786440 | tf_op jit(solution)/shard_map/ppermute | solution.py:280
  63.2 20.9 %collective-permute-start.9 = (bf16[64,16,128]{2,1,0:T(8,128)(2,1)S(1)}, bf16[64,16,128]{2,1,0:T(8,128)(2,1)S(1)}, u32[]{:S(2)}, u32[]{:S(2)}) collective-permute-start(bf16[64,16,128]{2,1,0:T(8,128)(2,1)S(1)} %add_convert_fusion.1.refs_0_), channel_id=1, source_target_pairs={{0,2},{1,3},{2,0},{3,1},{4,6},{5,7},{6,4},{7,5},{8,10},{9,11},{10,... | collective-permute-start | bytes 786440 | tf_op jit(solution)/shard_map/ppermute | solution.py:280
  67.6 16.5 %collective-permute-start.10 = (bf16[64,16,128]{2,1,0:T(8,128)(2,1)S(1)}, bf16[64,16,128]{2,1,0:T(8,128)(2,1)S(1)}, u32[]{:S(2)}, u32[]{:S(2)}) collective-permute-start(bf16[64,16,128]{2,1,0:T(8,128)(2,1)S(1)} %add_convert_fusion.1.refs_0_), channel_id=1, source_target_pairs={{0,3},{1,2},{2,1},{3,0},{4,7},{5,6},{6,5},{7,4},{8,11},{9,10},{10,... | collective-permute-start | bytes 786440 | tf_op jit(solution)/shard_map/ppermute | solution.py:280
  70.0 20.3 %collective-permute-start.21 = (bf16[64,16,128]{2,1,0:T(8,128)(2,1)S(1)}, bf16[64,16,128]{2,1,0:T(8,128)(2,1)S(1)}, u32[]{:S(2)}, u32[]{:S(2)}) collective-permute-start(bf16[64,16,128]{2,1,0:T(8,128)(2,1)S(1)} %add_convert_fusion.refs_0_), channel_id=1, source_target_pairs={{0,4},{4,0},{8,12},{12,8},{1,5},{5,1},{9,13},{13,9},{2,6},{6,2},{1... | collective-permute-start | bytes 786440 | tf_op jit(solution)/shard_map/ppermute | solution.py:280
  70.4 23.0 %collective-permute-start.22 = (bf16[64,16,128]{2,1,0:T(8,128)(2,1)S(1)}, bf16[64,16,128]{2,1,0:T(8,128)(2,1)S(1)}, u32[]{:S(2)}, u32[]{:S(2)}) collective-permute-start(bf16[64,16,128]{2,1,0:T(8,128)(2,1)S(1)} %add_convert_fusion.refs_0_), channel_id=1, source_target_pairs={{0,8},{4,12},{8,0},{12,4},{1,9},{5,13},{9,1},{13,5},{2,10},{6,14},... | collective-permute-start | bytes 786440 | tf_op jit(solution)/shard_map/ppermute | solution.py:280
  72.3 21.0 %collective-permute-start.23 = (bf16[64,16,128]{2,1,0:T(8,128)(2,1)S(1)}, bf16[64,16,128]{2,1,0:T(8,128)(2,1)S(1)}, u32[]{:S(2)}, u32[]{:S(2)}) collective-permute-start(bf16[64,16,128]{2,1,0:T(8,128)(2,1)S(1)} %add_convert_fusion.refs_0_), channel_id=1, source_target_pairs={{0,12},{4,8},{8,4},{12,0},{1,13},{5,9},{9,5},{13,1},{2,14},{6,10},... | collective-permute-start | bytes 786440 | tf_op jit(solution)/shard_map/ppermute | solution.py:280
  89.8 20.0 %collective-permute-start.11 = (bf16[64,16,128]{2,1,0:T(8,128)(2,1)S(1)}, bf16[64,16,128]{2,1,0:T(8,128)(2,1)S(1)}, u32[]{:S(2)}, u32[]{:S(2)}) collective-permute-start(bf16[64,16,128]{2,1,0:T(8,128)(2,1)S(1)} %get-tuple-element.30), channel_id=1, source_target_pairs={{0,4},{4,0},{8,12},{12,8},{1,5},{5,1},{9,13},{13,9},{2,6},{6,2},{1... | collective-permute-start | bytes 786440 | tf_op jit(solution)/shard_map/ppermute | solution.py:277
  90.3 19.6 %collective-permute-start.12 = (bf16[64,16,128]{2,1,0:T(8,128)(2,1)S(1)}, bf16[64,16,128]{2,1,0:T(8,128)(2,1)S(1)}, u32[]{:S(2)}, u32[]{:S(2)}) collective-permute-start(bf16[64,16,128]{2,1,0:T(8,128)(2,1)S(1)} %get-tuple-element.31), channel_id=1, source_target_pairs={{0,8},{4,12},{8,0},{12,4},{1,9},{5,13},{9,1},{13,5},{2,10},{6,14},... | collective-permute-start | bytes 786440 | tf_op jit(solution)/shard_map/ppermute | solution.py:277
  90.3 23.2 %collective-permute-start.13 = (bf16[64,16,128]{2,1,0:T(8,128)(2,1)S(1)}, bf16[64,16,128]{2,1,0:T(8,128)(2,1)S(1)}, u32[]{:S(2)}, u32[]{:S(2)}) collective-permute-start(bf16[64,16,128]{2,1,0:T(8,128)(2,1)S(1)} %get-tuple-element.32), channel_id=1, source_target_pairs={{0,12},{4,8},{8,4},{12,0},{1,13},{5,9},{9,5},{13,1},{2,14},{6,10},... | collective-permute-start | bytes 786440 | tf_op jit(solution)/shard_map/ppermute | solution.py:277
  100.8 33.4 %collective-permute-start.24 = (bf16[64,16,128]{2,1,0:T(8,128)(2,1)S(1)}, bf16[64,16,128]{2,1,0:T(8,128)(2,1)S(1)}, u32[]{:S(2)}, u32[]{:S(2)}) collective-permute-start(bf16[64,16,128]{2,1,0:T(8,128)(2,1)S(1)} %get-tuple-element.41), channel_id=1, source_target_pairs={{0,0},{1,4},{2,8},{3,12},{4,1},{5,5},{6,9},{7,13},{8,2},{9,6},{10,... | collective-permute-start | bytes 786440 | tf_op jit(solution)/shard_map/ppermute | solution.py:293
  107.2 26.9 %collective-permute-start.25 = (bf16[64,16,128]{2,1,0:T(8,128)(2,1)S(1)}, bf16[64,16,128]{2,1,0:T(8,128)(2,1)S(1)}, u32[]{:S(2)}, u32[]{:S(2)}) collective-permute-start(bf16[64,16,128]{2,1,0:T(8,128)(2,1)S(1)} %get-tuple-element.42), channel_id=1, source_target_pairs={{0,4},{1,0},{2,12},{3,8},{4,5},{5,1},{6,13},{7,9},{8,6},{9,2},{10,... | collective-permute-start | bytes 786440 | tf_op jit(solution)/shard_map/ppermute | solution.py:293
  109.8 24.4 %collective-permute-start.26 = (bf16[64,16,128]{2,1,0:T(8,128)(2,1)S(1)}, bf16[64,16,128]{2,1,0:T(8,128)(2,1)S(1)}, u32[]{:S(2)}, u32[]{:S(2)}) collective-permute-start(bf16[64,16,128]{2,1,0:T(8,128)(2,1)S(1)} %get-tuple-element.43), channel_id=1, source_target_pairs={{0,8},{1,12},{2,0},{3,4},{4,9},{5,13},{6,1},{7,5},{8,10},{9,14},{1... | collective-permute-start | bytes 786440 | tf_op jit(solution)/shard_map/ppermute | solution.py:293
  109.8 59.8 %collective-permute-start.27 = (bf16[64,16,128]{2,1,0:T(8,128)(2,1)S(1)}, bf16[64,16,128]{2,1,0:T(8,128)(2,1)S(1)}, u32[]{:S(2)}, u32[]{:S(2)}) collective-permute-start(bf16[64,16,128]{2,1,0:T(8,128)(2,1)S(1)} %get-tuple-element.44), channel_id=1, source_target_pairs={{0,12},{1,8},{2,4},{3,0},{4,13},{5,9},{6,5},{7,1},{8,14},{9,10},{1... | collective-permute-start | bytes 786440 | tf_op jit(solution)/shard_map/ppermute | solution.py:293
where the time goes:
time: 171 us
  waiting for transfers between devices  103 us (60%)
  starting transfers between devices  37.2 us (22%)
  Pallas kernels  27.6 us (16%)
  local copies, waits for them, and re-layouts  1.74 us (1%)
    ppermute x4, waiting for transfers between devices, local(): lax.ppermute(out_b[m], both, [(a * size + b, (b ^ m) * size + a) for a in...  56.1 us
    ppermute x4, waiting for transfers between devices, local(): lax.ppermute(pay_b, both, [(a, a * size + (a ^ k)) for a in range(size)])  25.9 us
    pallas_call x2, Pallas kernels, product_two(): pl.pallas_call(functools.partial(product_two_kernel, by_rows, here, block...  13.1 us
    ppermute x4, starting transfers between devices, local(): lax.ppermute(out_b[m], both, [(a * size + b, (b ^ m) * size + a) for a in...  12.6 us
    ppermute x9, starting transfers between devices, scatter(): lax.ppermute(sends[k], axis, swaps(size, k))  11.5 us
    ppermute x6, waiting for transfers between devices, spread(): lax.ppermute(own, axis, swaps(size, k))  10.5 us
    ppermute x6, starting transfers between devices, spread(): lax.ppermute(own, axis, swaps(size, k))  6.64 us
    ppermute x9, waiting for transfers between devices, scatter(): lax.ppermute(sends[k], axis, swaps(size, k))  5.66 us
  transfers between devices with their start and end apart: 28, of which 7 were waited for; matrix products, arithmetic and copies ran while one was open for 2% of the time, Pallas kernels for 14%

commit v1 on v0

--- a/solution.py
+++ b/solution.py
@@ -43,6 +43,29 @@
         cost_estimate=pl.CostEstimate(flops=4_000_000, bytes_accessed=25_000_000, transcendentals=0),
         name="assemble",
     )(*parts)
+
+
+def pick_kernel(*refs):
+    blocks = len(refs) // 2
+    a, b = lax.axis_index("gy"), lax.axis_index("gz")
+    for m in range(blocks):
+        for k in range(blocks):
+
+            @pl.when(a ^ b ^ k == m)
+            def _(k=k, m=m):
+                refs[blocks + k][...] = refs[m][...]
+
+
+def pick(values):
+    return pl.pallas_call(
+        pick_kernel,
+        out_shape=[jax.ShapeDtypeStruct(value.shape, value.dtype) for value in values],
+        in_specs=[pl.BlockSpec(memory_space=VMEM)] * len(values),
+        out_specs=[pl.BlockSpec(memory_space=VMEM)] * len(values),
+        compiler_params=limit(8),
+        cost_estimate=pl.CostEstimate(flops=1_000_000, bytes_accessed=2_000_000, transcendentals=0),
+        name="pick",
+    )(*values)
 
 
 def swaps(size, step):
@@ -152,7 +175,7 @@
     slab, slots = slab_ref.shape[:2]
     rows = left_ref.shape[2]
     for k in range(blocks):
-        left_ref[a ^ b ^ k] = round_refs[k][...]
+        left_ref[k if by_rows else a ^ b ^ k] = round_refs[k][...]
     extra = jnp.where(a == b, 3.0, 0.0).astype(jnp.float32)
 
     def left_of(p):
@@ -264,13 +287,14 @@
     pay_a, pay_b = payload(0), payload(rows)
     both = ("gy", "gz")
     shifts = [[((i + t) % parts, i) for i in range(parts)] for t in range(1, parts)]
+    others = [lax.ppermute(columns_here, "gx", s) for s in shifts]
+    moved = [lax.ppermute(tiles_here, "gx", s) for s in shifts]
     left_a = [pay_a] + [lax.ppermute(pay_a, "gy", [(0, k)]) for k in range(1, size)]
-    columns = jnp.concatenate([columns_here] + [lax.ppermute(columns_here, "gx", s) for s in shifts], axis=0)
-    inverse = invert(columns)
-    moved = [lax.ppermute(tiles_here, "gx", s) for s in shifts]
     left_b = [
         lax.ppermute(pay_b, both, [(a, a * size + (a ^ k)) for a in range(size)]) for k in range(size)
     ]
+    columns = jnp.concatenate([columns_here] + others, axis=0)
+    inverse = invert(columns)
     tiles = assemble([tiles_here] + moved)
 
     def scatter(sends, axis):
@@ -289,14 +313,9 @@
     rounded_b = spread(own_b, "gy")
     rounded_a = spread(own_a, "gz")
     out_b = product_two(True, columns, rounded_b, tiles, here)
-    got_b = [
-        lax.ppermute(
-            out_b[m],
-            both,
-            [(a * size + b, (b ^ m) * size + a) for a in range(size) for b in range(size)],
-        )
-        for m in range(size)
-    ]
+    crossed = scatter(out_b, "gy")
+    picked = pick(crossed)
+    got_b = scatter(picked, "gz")
     out_a = product_two(False, inverse, rounded_a, tiles, here)
     got_a = scatter(out_a, "gy")
     return finish(got_a, got_b, here)

time: 171 us -> 120 us (0.70)
  the two profiles are of different devices: /device:TPU:4 before, /device:TPU:0 now
where the time goes in v1:
time: 120 us; the launch traced here: 119 us
  starting transfers between devices  46.8 us (39%)
  waiting for transfers between devices  41.1 us (34%)
  Pallas kernels  27.7 us (23%)
  local copies, waits for them, and re-layouts  1.74 us (1%)
  other arithmetic  1.33 us (1%)
    ppermute x15, waiting for transfers between devices, scatter(): lax.ppermute(sends[k], axis, swaps(size, k))  34.7 us
    ppermute x15, starting transfers between devices, scatter(): lax.ppermute(sends[k], axis, swaps(size, k))  17.3 us
    ppermute x4, starting transfers between devices, local(): lax.ppermute(pay_b, both, [(a, a * size + (a ^ k)) for a in range(size)])  13.8 us
    pallas_call x2, Pallas kernels, product_two(): pl.pallas_call(functools.partial(product_two_kernel, by_rows, here, block...  13.1 us
    ppermute x6, starting transfers between devices, spread(): lax.ppermute(own, axis, swaps(size, k))  8 us
    ppermute x3, starting transfers between devices, local(): lax.ppermute(pay_a, 'gy', [(0, k)])  6.97 us
    ppermute x6, waiting for transfers between devices, spread(): lax.ppermute(own, axis, swaps(size, k))  6.19 us
    pallas_call x1, Pallas kernels, assemble(): pl.pallas_call(functools.partial(assemble_kernel, len(parts)), out_shape=...  4.63 us
  transfers between devices with their start and end apart: 30, of which 7 were waited for; matrix products, arithmetic and copies ran while one was open for 3% of the time, Pallas kernels for 21%

profile of v1, /device:TPU:0, one launch (start us, length us, event | category | flops | bytes accessed | tf_op | source)
XLA Modules:
  0.0 118.9 jit_solution(5178512714692301936)
XLA Ops:
  0.0 0.5 collective-permute-start.1
  0.5 0.9 slice.17
  1.4 0.8 fusion
  2.3 0.1 pad_maximum_fusion.1
  2.4 4.4 %collective-permute-start.2 = (bf16[400,128]{1,0:T(8,128)(2,1)S(1)}, bf16[400,128]{1,0:T(8,128)(2,1)S(1)}, u32[]{:S(2)}, u32[]{:S(2)}) collective-permute-start(bf16[400,128]{1,0:T(8,128)(2,1)S(1)} %get-tuple-element.56.refs_0_), channel_id=1, source_target_pairs={{0,4},{1,5},{2,6},{3,7},{16,20},{17,21},{18,22},{19,23}} | collective-permute-start | bytes 307208 | tf_op jit(solution)/shard_map/ppermute | solution.py:292
  6.8 1.3 %collective-permute-start.3 = (bf16[400,128]{1,0:T(8,128)(2,1)S(1)}, bf16[400,128]{1,0:T(8,128)(2,1)S(1)}, u32[]{:S(2)}, u32[]{:S(2)}) collective-permute-start(bf16[400,128]{1,0:T(8,128)(2,1)S(1)} %get-tuple-element.56.refs_0_), channel_id=1, source_target_pairs={{0,8},{1,9},{2,10},{3,11},{16,24},{17,25},{18,26},{19,27}} | collective-permute-start | bytes 307208 | tf_op jit(solution)/shard_map/ppermute | solution.py:292
  8.1 0.7 copy.10
  8.8 0.2 collective-permute-start
  9.0 1.3 %collective-permute-start.4 = (bf16[400,128]{1,0:T(8,128)(2,1)S(1)}, bf16[400,128]{1,0:T(8,128)(2,1)S(1)}, u32[]{:S(2)}, u32[]{:S(2)}) collective-permute-start(bf16[400,128]{1,0:T(8,128)(2,1)S(1)} %get-tuple-element.56.refs_0_), channel_id=1, source_target_pairs={{0,12},{1,13},{2,14},{3,15},{16,28},{17,29},{18,30},{19,31}} | collective-permute-start | bytes 307208 | tf_op jit(solution)/shard_map/ppermute | solution.py:292
  10.3 0.2 collective-permute-done
  10.5 0.7 collective-permute-start.14
  11.2 7.6 %collective-permute-start.15 = (bf16[400,128]{1,0:T(8,128)(2,1)S(1)}, bf16[400,128]{1,0:T(8,128)(2,1)S(1)}, u32[]{:S(2)}, u32[]{:S(2)}) collective-permute-start(bf16[400,128]{1,0:T(8,128)(2,1)S(1)} %get-tuple-element.55), channel_id=1, source_target_pairs={{0,1},{1,4},{2,11},{3,14},{16,17},{17,20},{18,27},{19,30}} | collective-permute-start | bytes 307208 | tf_op jit(solution)/shard_map/ppermute | solution.py:294
  18.8 2.7 %collective-permute-start.16 = (bf16[400,128]{1,0:T(8,128)(2,1)S(1)}, bf16[400,128]{1,0:T(8,128)(2,1)S(1)}, u32[]{:S(2)}, u32[]{:S(2)}) collective-permute-start(bf16[400,128]{1,0:T(8,128)(2,1)S(1)} %get-tuple-element.55), channel_id=1, source_target_pairs={{0,2},{1,7},{2,8},{3,13},{16,18},{17,23},{18,24},{19,29}} | collective-permute-start | bytes 307208 | tf_op jit(solution)/shard_map/ppermute | solution.py:294
  21.5 2.9 %collective-permute-start.17 = (bf16[400,128]{1,0:T(8,128)(2,1)S(1)}, bf16[400,128]{1,0:T(8,128)(2,1)S(1)}, u32[]{:S(2)}, u32[]{:S(2)}) collective-permute-start(bf16[400,128]{1,0:T(8,128)(2,1)S(1)} %get-tuple-element.55), channel_id=1, source_target_pairs={{0,3},{1,6},{2,9},{3,12},{16,19},{17,22},{18,25},{19,28}} | collective-permute-start | bytes 307208 | tf_op jit(solution)/shard_map/ppermute | solution.py:294
  24.4 0.1 pad_add_fusion
  24.5 0.1 copy.5.cols_ref.index_ref
  24.6 4.3 %invert.1.index_ref = s32[64,6]{1,0:T(8,128)S(1)} custom-call(s32[64,6]{1,0:T(8,128)S(1)} %copy.5.cols_ref.index_ref), custom_call_target="tpu_custom_call" | custom-call | flops 4000000 | bytes 4096 | tf_op jit(solution)/shard_map/invert/pallas_call | solution.py:93
  28.9 4.6 %assemble.1.slab_ref = bf16[64,6,128,128]{3,2,1,0:T(8,128)(2,1)S(1)} custom-call(bf16[32,6,128,128]{3,2,1,0:T(8,128)(2,1)} %bitcast.8, bf16[32,6,128,128]{3,2,1,0:T(8,128)(2,1)} %copy-done), custom_call_target="tpu_custom_call" | custom-call | flops 4000000 | bytes 25000000 | tf_op jit(solution)/shard_map/assemble/pallas_call | solution.py:36
  33.5 2.3 %one_columns.1 = (bf16[64,16,128]{2,1,0:T(8,128)(2,1)S(1)}, bf16[64,16,128]{2,1,0:T(8,128)(2,1)S(1)}, bf16[64,16,128]{2,1,0:T(8,128)(2,1)S(1)}, bf16[64,16,128]{2,1,0:T(8,128)(2,1)S(1)}) custom-call(s32[64,6]{1,0:T(8,128)S(1)} %invert.1.index_ref, bf16[64,6,128,128]{3,2,1,0:T(8,128)(2,1)S(1)} %assemble.1.slab_ref, ...), custom_call_target="tpu_custom_call" | custom-call | flops 12000000 | bytes 4000000 | tf_op jit(solution)/shard_map/one_columns/pallas_call | solution.py:155
  35.9 1.8 %one_rows.1 = (bf16[64,16,128]{2,1,0:T(8,128)(2,1)S(1)}, bf16[64,16,128]{2,1,0:T(8,128)(2,1)S(1)}, bf16[64,16,128]{2,1,0:T(8,128)(2,1)S(1)}, bf16[64,16,128]{2,1,0:T(8,128)(2,1)S(1)}) custom-call(s32[64,6]{1,0:T(8,128)S(1)} %copy.5.cols_ref.index_ref, bf16[64,6,128,128]{3,2,1,0:T(8,128)(2,1)S(1)} %assemble.1.slab_ref, ...), custom_call_target="tpu_custom_call" | custom-call | flops 12000000 | bytes 4000000 | tf_op jit(solution)/shard_map/one_rows/pallas_call | solution.py:155
  37.9 3.4 %collective-permute-start.18 = (bf16[64,16,128]{2,1,0:T(8,128)(2,1)S(1)}, bf16[64,16,128]{2,1,0:T(8,128)(2,1)S(1)}, u32[]{:S(2)}, u32[]{:S(2)}) collective-permute-start(bf16[64,16,128]{2,1,0:T(8,128)(2,1)S(1)} %get-tuple-element.42), channel_id=1, source_target_pairs={{0,4},{4,0},{8,12},{12,8},{1,5},{5,1},{9,13},{13,9},{2,6},{6,2},{1... | collective-permute-start | bytes 786440 | tf_op jit(solution)/shard_map/ppermute | solution.py:301
  41.3 0.7 collective-permute-start.7
  42.0 5.9 %collective-permute-done.20 = bf16[64,16,128]{2,1,0:T(8,128)(2,1)S(1)} collective-permute-done((bf16[64,16,128]{2,1,0:T(8,128)(2,1)S(1)}, bf16[64,16,128]{2,1,0:T(8,128)(2,1)S(1)}, u32[]{:S(2)}, u32[]{:S(2)}) %collective-permute-start.20) | collective-permute-done | bytes 262176 | tf_op jit(solution)/shard_map/ppermute | solution.py:301
  47.9 3.4 %collective-permute-done.19 = bf16[64,16,128]{2,1,0:T(8,128)(2,1)S(1)} collective-permute-done((bf16[64,16,128]{2,1,0:T(8,128)(2,1)S(1)}, bf16[64,16,128]{2,1,0:T(8,128)(2,1)S(1)}, u32[]{:S(2)}, u32[]{:S(2)}) %collective-permute-start.19) | collective-permute-done | bytes 262176 | tf_op jit(solution)/shard_map/ppermute | solution.py:301
  51.3 0.2 add_convert_fusion.refs_0_
  51.4 0.3 collective-permute-start.21
  51.8 1.4 %collective-permute-start.22 = (bf16[64,16,128]{2,1,0:T(8,128)(2,1)S(1)}, bf16[64,16,128]{2,1,0:T(8,128)(2,1)S(1)}, u32[]{:S(2)}, u32[]{:S(2)}) collective-permute-start(bf16[64,16,128]{2,1,0:T(8,128)(2,1)S(1)} %add_convert_fusion.refs_0_), channel_id=1, source_target_pairs={{0,8},{4,12},{8,0},{12,4},{1,9},{5,13},{9,1},{13,5},{2,10},{6,14},... | collective-permute-start | bytes 786440 | tf_op jit(solution)/shard_map/ppermute | solution.py:304
  53.2 1.8 %collective-permute-start.23 = (bf16[64,16,128]{2,1,0:T(8,128)(2,1)S(1)}, bf16[64,16,128]{2,1,0:T(8,128)(2,1)S(1)}, u32[]{:S(2)}, u32[]{:S(2)}) collective-permute-start(bf16[64,16,128]{2,1,0:T(8,128)(2,1)S(1)} %add_convert_fusion.refs_0_), channel_id=1, source_target_pairs={{0,12},{4,8},{8,4},{12,0},{1,13},{5,9},{9,5},{13,1},{2,14},{6,10},... | collective-permute-start | bytes 786440 | tf_op jit(solution)/shard_map/ppermute | solution.py:304
  55.0 8.4 %collective-permute-done.6 = bf16[64,16,128]{2,1,0:T(8,128)(2,1)S(1)} collective-permute-done((bf16[64,16,128]{2,1,0:T(8,128)(2,1)S(1)}, bf16[64,16,128]{2,1,0:T(8,128)(2,1)S(1)}, u32[]{:S(2)}, u32[]{:S(2)}) %collective-permute-start.6) | collective-permute-done | bytes 262176 | tf_op jit(solution)/shard_map/ppermute | solution.py:301
  63.4 0.1 add_convert_fusion.1.refs_0_
  63.6 3.2 %collective-permute-start.9 = (bf16[64,16,128]{2,1,0:T(8,128)(2,1)S(1)}, bf16[64,16,128]{2,1,0:T(8,128)(2,1)S(1)}, u32[]{:S(2)}, u32[]{:S(2)}) collective-permute-start(bf16[64,16,128]{2,1,0:T(8,128)(2,1)S(1)} %add_convert_fusion.1.refs_0_), channel_id=1, source_target_pairs={{0,2},{1,3},{2,0},{3,1},{4,6},{5,7},{6,4},{7,5},{8,10},{9,11},{10,... | collective-permute-start | bytes 786440 | tf_op jit(solution)/shard_map/ppermute | solution.py:304
  66.8 1.2 collective-permute-start.10
  68.0 7.5 %two_rows.1 = (bf16[64,16,128]{2,1,0:T(8,128)(2,1)S(1)}, bf16[64,16,128]{2,1,0:T(8,128)(2,1)S(1)}, bf16[64,16,128]{2,1,0:T(8,128)(2,1)S(1)}, bf16[64,16,128]{2,1,0:T(8,128)(2,1)S(1)}) custom-call(s32[64,6]{1,0:T(8,128)S(1)} %copy.5.cols_ref.index_ref, bf16[64,6,128,128]{3,2,1,0:T(8,128)(2,1)S(1)} %assemble.1.slab_ref, ...), custom_call_target="tpu_custom_call" | custom-call | flops 30000000 | bytes 12000000 | tf_op jit(solution)/shard_map/two_rows/pallas_call | solution.py:220
  75.5 0.3 collective-permute-start.24
  75.8 0.6 collective-permute-start.25
  76.4 2.6 %collective-permute-start.26 = (bf16[64,16,128]{2,1,0:T(8,128)(2,1)S(1)}, bf16[64,16,128]{2,1,0:T(8,128)(2,1)S(1)}, u32[]{:S(2)}, u32[]{:S(2)}) collective-permute-start(bf16[64,16,128]{2,1,0:T(8,128)(2,1)S(1)} %get-tuple-element.48), channel_id=1, source_target_pairs={{0,12},{4,8},{8,4},{12,0},{1,13},{5,9},{9,5},{13,1},{2,14},{6,10},... | collective-permute-start | bytes 786440 | tf_op jit(solution)/shard_map/ppermute | solution.py:301
  79.0 6.2 %collective-permute-done.9.refs_2_ = bf16[64,16,128]{2,1,0:T(8,128)(2,1)S(1)} collective-permute-done((bf16[64,16,128]{2,1,0:T(8,128)(2,1)S(1)}, bf16[64,16,128]{2,1,0:T(8,128)(2,1)S(1)}, u32[]{:S(2)}, u32[]{:S(2)}) %collective-permute-start.9) | collective-permute-done | bytes 262176 | tf_op jit(solution)/shard_map/ppermute | solution.py:304
  85.2 5.7 %two_columns.1 = (bf16[64,16,128]{2,1,0:T(8,128)(2,1)S(1)}, bf16[64,16,128]{2,1,0:T(8,128)(2,1)S(1)}, bf16[64,16,128]{2,1,0:T(8,128)(2,1)S(1)}, bf16[64,16,128]{2,1,0:T(8,128)(2,1)S(1)}) custom-call(s32[64,6]{1,0:T(8,128)S(1)} %invert.1.index_ref, bf16[64,6,128,128]{3,2,1,0:T(8,128)(2,1)S(1)} %assemble.1.slab_ref, ...), custom_call_target="tpu_custom_call" | custom-call | flops 30000000 | bytes 12000000 | tf_op jit(solution)/shard_map/two_columns/pallas_call | solution.py:220
  90.9 0.3 collective-permute-start.11
  91.2 0.7 collective-permute-start.12
  91.9 2.6 %collective-permute-start.13 = (bf16[64,16,128]{2,1,0:T(8,128)(2,1)S(1)}, bf16[64,16,128]{2,1,0:T(8,128)(2,1)S(1)}, u32[]{:S(2)}, u32[]{:S(2)}) collective-permute-start(bf16[64,16,128]{2,1,0:T(8,128)(2,1)S(1)} %get-tuple-element.36), channel_id=1, source_target_pairs={{0,12},{4,8},{8,4},{12,0},{1,13},{5,9},{9,5},{13,1},{2,14},{6,10},... | collective-permute-start | bytes 786440 | tf_op jit(solution)/shard_map/ppermute | solution.py:301
  94.4 0.1 pick.1
  94.6 3.5 %collective-permute-start.27 = (bf16[64,16,128]{2,1,0:T(8,128)(2,1)S(1)}, bf16[64,16,128]{2,1,0:T(8,128)(2,1)S(1)}, u32[]{:S(2)}, u32[]{:S(2)}) collective-permute-start(bf16[64,16,128]{2,1,0:T(8,128)(2,1)S(1)} %get-tuple-element.50), channel_id=1, source_target_pairs={{0,1},{1,0},{2,3},{3,2},{4,5},{5,4},{6,7},{7,6},{8,9},{9,8},{10,11... | collective-permute-start | bytes 786440 | tf_op jit(solution)/shard_map/ppermute | solution.py:301
  98.1 1.0 collective-permute-start.28
  99.1 1.4 %collective-permute-start.29 = (bf16[64,16,128]{2,1,0:T(8,128)(2,1)S(1)}, bf16[64,16,128]{2,1,0:T(8,128)(2,1)S(1)}, u32[]{:S(2)}, u32[]{:S(2)}) collective-permute-start(bf16[64,16,128]{2,1,0:T(8,128)(2,1)S(1)} %get-tuple-element.52), channel_id=1, source_target_pairs={{0,3},{1,2},{2,1},{3,0},{4,7},{5,6},{6,5},{7,4},{8,11},{9,10},{10,... | collective-permute-start | bytes 786440 | tf_op jit(solution)/shard_map/ppermute | solution.py:301
  100.5 4.2 %collective-permute-done.27.refs_5_ = bf16[64,16,128]{2,1,0:T(8,128)(2,1)S(1)} collective-permute-done((bf16[64,16,128]{2,1,0:T(8,128)(2,1)S(1)}, bf16[64,16,128]{2,1,0:T(8,128)(2,1)S(1)}, u32[]{:S(2)}, u32[]{:S(2)}) %collective-permute-start.27) | collective-permute-done | bytes 262176 | tf_op jit(solution)/shard_map/ppermute | solution.py:301
  104.8 12.8 %collective-permute-done.28.refs_6_ = bf16[64,16,128]{2,1,0:T(8,128)(2,1)S(1)} collective-permute-done((bf16[64,16,128]{2,1,0:T(8,128)(2,1)S(1)}, bf16[64,16,128]{2,1,0:T(8,128)(2,1)S(1)}, u32[]{:S(2)}, u32[]{:S(2)}) %collective-permute-start.28) | collective-permute-done | bytes 262176 | tf_op jit(solution)/shard_map/ppermute | solution.py:301
  117.5 1.4 %finish.1 = f32[32,8192]{1,0:T(8,128)} custom-call(bf16[64,16,128]{2,1,0:T(8,128)(2,1)S(1)} %get-tuple-element.33.refs_0_, bf16[64,16,128]{2,1,0:T(8,128)(2,1)S(1)} %collective-permute-done.11.refs_1_, bf16[64,16,128]{2,1,0:T(8,128)(2,1)S(1)} %collective-permute-done.12.refs_2_, bf16[64,16,128]{2,1,0:T(8,128)(2,1)S(1)} %collective-permute-done.13.refs_3_, ...), custom_call_target="tpu_custom_call" | custom-call | tf_op jit(solution)/shard_map/finish/pallas_call | solution.py:254
  (32 shorter events, 0.3 us)
Async XLA Ops:
  0.0 21.5 %collective-permute-start.1 = (bf16[32,6,128,128]{3,2,1,0:T(8,128)(2,1)}, bf16[32,6,128,128]{3,2,1,0:T(8,128)(2,1)S(1)}, u32[]{:S(2)}, u32[]{:S(2)}) collective-permute-start(bf16[32,6,128,128]{3,2,1,0:T(8,128)(2,1)} %bitcast.7), channel_id=1, source_target_pairs={{16,0},{0,16},{17,1},{1,17},{18,2},{2,18},{19,3},{3,19},{20,4},{4,... | collective-permute-start | bytes 18874376 | tf_op jit(solution)/shard_map/ppermute | solution.py:291
  2.4 8.8 %collective-permute-start.2 = (bf16[400,128]{1,0:T(8,128)(2,1)S(1)}, bf16[400,128]{1,0:T(8,128)(2,1)S(1)}, u32[]{:S(2)}, u32[]{:S(2)}) collective-permute-start(bf16[400,128]{1,0:T(8,128)(2,1)S(1)} %get-tuple-element.56.refs_0_), channel_id=1, source_target_pairs={{0,4},{1,5},{2,6},{3,7},{16,20},{17,21},{18,22},{19,23}} | collective-permute-start | bytes 307208 | tf_op jit(solution)/shard_map/ppermute | solution.py:292
  6.8 11.9 %collective-permute-start.3 = (bf16[400,128]{1,0:T(8,128)(2,1)S(1)}, bf16[400,128]{1,0:T(8,128)(2,1)S(1)}, u32[]{:S(2)}, u32[]{:S(2)}) collective-permute-start(bf16[400,128]{1,0:T(8,128)(2,1)S(1)} %get-tuple-element.56.refs_0_), channel_id=1, source_target_pairs={{0,8},{1,9},{2,10},{3,11},{16,24},{17,25},{18,26},{19,27}} | collective-permute-start | bytes 307208 | tf_op jit(solution)/shard_map/ppermute | solution.py:292
  8.8 1.7 %collective-permute-start = (s32[32,6]{0,1:T(8,128)S(1)}, s32[32,6]{0,1:T(8,128)S(1)}, u32[]{:S(2)}, u32[]{:S(2)}) collective-permute-start(s32[32,6]{0,1:T(8,128)S(1)} %bitcast.12), channel_id=1, source_target_pairs={{16,0},{0,16},{17,1},{1,17},{18,2},{2,18},{19,3},{3,19},{20,4},{4,... | collective-permute-start | bytes 2312 | tf_op jit(solution)/shard_map/ppermute | solution.py:290
  9.0 24.5 %collective-permute-start.4 = (bf16[400,128]{1,0:T(8,128)(2,1)S(1)}, bf16[400,128]{1,0:T(8,128)(2,1)S(1)}, u32[]{:S(2)}, u32[]{:S(2)}) collective-permute-start(bf16[400,128]{1,0:T(8,128)(2,1)S(1)} %get-tuple-element.56.refs_0_), channel_id=1, source_target_pairs={{0,12},{1,13},{2,14},{3,15},{16,28},{17,29},{18,30},{19,31}} | collective-permute-start | bytes 307208 | tf_op jit(solution)/shard_map/ppermute | solution.py:292
  10.5 25.3 %collective-permute-start.14 = (bf16[400,128]{1,0:T(8,128)(2,1)S(1)}, bf16[400,128]{1,0:T(8,128)(2,1)S(1)}, u32[]{:S(2)}, u32[]{:S(2)}) collective-permute-start(bf16[400,128]{1,0:T(8,128)(2,1)S(1)} %get-tuple-element.55), channel_id=1, source_target_pairs={{0,0},{1,5},{2,10},{3,15},{16,16},{17,21},{18,26},{19,31}} | collective-permute-start | bytes 307208 | tf_op jit(solution)/shard_map/ppermute | solution.py:294
  11.2 24.7 %collective-permute-start.15 = (bf16[400,128]{1,0:T(8,128)(2,1)S(1)}, bf16[400,128]{1,0:T(8,128)(2,1)S(1)}, u32[]{:S(2)}, u32[]{:S(2)}) collective-permute-start(bf16[400,128]{1,0:T(8,128)(2,1)S(1)} %get-tuple-element.55), channel_id=1, source_target_pairs={{0,1},{1,4},{2,11},{3,14},{16,17},{17,20},{18,27},{19,30}} | collective-permute-start | bytes 307208 | tf_op jit(solution)/shard_map/ppermute | solution.py:294
  18.8 17.1 %collective-permute-start.16 = (bf16[400,128]{1,0:T(8,128)(2,1)S(1)}, bf16[400,128]{1,0:T(8,128)(2,1)S(1)}, u32[]{:S(2)}, u32[]{:S(2)}) collective-permute-start(bf16[400,128]{1,0:T(8,128)(2,1)S(1)} %get-tuple-element.55), channel_id=1, source_target_pairs={{0,2},{1,7},{2,8},{3,13},{16,18},{17,23},{18,24},{19,29}} | collective-permute-start | bytes 307208 | tf_op jit(solution)/shard_map/ppermute | solution.py:294
  21.5 2.9 %copy-start = (bf16[32,6,128,128]{3,2,1,0:T(8,128)(2,1)}, bf16[32,6,128,128]{3,2,1,0:T(8,128)(2,1)S(1)}, u32[]{:S(2)}) copy-start(bf16[32,6,128,128]{3,2,1,0:T(8,128)(2,1)S(1)} %collective-permute-done.1.refs_1_) | copy-start | bytes 18874372
  21.5 14.3 %collective-permute-start.17 = (bf16[400,128]{1,0:T(8,128)(2,1)S(1)}, bf16[400,128]{1,0:T(8,128)(2,1)S(1)}, u32[]{:S(2)}, u32[]{:S(2)}) collective-permute-start(bf16[400,128]{1,0:T(8,128)(2,1)S(1)} %get-tuple-element.55), channel_id=1, source_target_pairs={{0,3},{1,6},{2,9},{3,12},{16,19},{17,22},{18,25},{19,28}} | collective-permute-start | bytes 307208 | tf_op jit(solution)/shard_map/ppermute | solution.py:294
  37.7 10.1 %collective-permute-start.20 = (bf16[64,16,128]{2,1,0:T(8,128)(2,1)S(1)}, bf16[64,16,128]{2,1,0:T(8,128)(2,1)S(1)}, u32[]{:S(2)}, u32[]{:S(2)}) collective-permute-start(bf16[64,16,128]{2,1,0:T(8,128)(2,1)S(1)} %get-tuple-element.44), channel_id=1, source_target_pairs={{0,12},{4,8},{8,4},{12,0},{1,13},{5,9},{9,5},{13,1},{2,14},{6,10},... | collective-permute-start | bytes 786440 | tf_op jit(solution)/shard_map/ppermute | solution.py:301
  37.8 13.5 %collective-permute-start.19 = (bf16[64,16,128]{2,1,0:T(8,128)(2,1)S(1)}, bf16[64,16,128]{2,1,0:T(8,128)(2,1)S(1)}, u32[]{:S(2)}, u32[]{:S(2)}) collective-permute-start(bf16[64,16,128]{2,1,0:T(8,128)(2,1)S(1)} %get-tuple-element.43), channel_id=1, source_target_pairs={{0,8},{4,12},{8,0},{12,4},{1,9},{5,13},{9,1},{13,5},{2,10},{6,14},... | collective-permute-start | bytes 786440 | tf_op jit(solution)/shard_map/ppermute | solution.py:301
  37.9 13.4 %collective-permute-start.18 = (bf16[64,16,128]{2,1,0:T(8,128)(2,1)S(1)}, bf16[64,16,128]{2,1,0:T(8,128)(2,1)S(1)}, u32[]{:S(2)}, u32[]{:S(2)}) collective-permute-start(bf16[64,16,128]{2,1,0:T(8,128)(2,1)S(1)} %get-tuple-element.42), channel_id=1, source_target_pairs={{0,4},{4,0},{8,12},{12,8},{1,5},{5,1},{9,13},{13,9},{2,6},{6,2},{1... | collective-permute-start | bytes 786440 | tf_op jit(solution)/shard_map/ppermute | solution.py:301
  41.3 11.9 %collective-permute-start.7 = (bf16[64,16,128]{2,1,0:T(8,128)(2,1)S(1)}, bf16[64,16,128]{2,1,0:T(8,128)(2,1)S(1)}, u32[]{:S(2)}, u32[]{:S(2)}) collective-permute-start(bf16[64,16,128]{2,1,0:T(8,128)(2,1)S(1)} %get-tuple-element.32), channel_id=1, source_target_pairs={{0,3},{1,2},{2,1},{3,0},{4,7},{5,6},{6,5},{7,4},{8,11},{9,10},{10,... | collective-permute-start | bytes 786440 | tf_op jit(solution)/shard_map/ppermute | solution.py:301
  42.0 21.4 %collective-permute-start.6 = (bf16[64,16,128]{2,1,0:T(8,128)(2,1)S(1)}, bf16[64,16,128]{2,1,0:T(8,128)(2,1)S(1)}, u32[]{:S(2)}, u32[]{:S(2)}) collective-permute-start(bf16[64,16,128]{2,1,0:T(8,128)(2,1)S(1)} %get-tuple-element.31), channel_id=1, source_target_pairs={{0,2},{1,3},{2,0},{3,1},{4,6},{5,7},{6,4},{7,5},{8,10},{9,11},{10,... | collective-permute-start | bytes 786440 | tf_op jit(solution)/shard_map/ppermute | solution.py:301
  47.9 15.5 %collective-permute-start.5 = (bf16[64,16,128]{2,1,0:T(8,128)(2,1)S(1)}, bf16[64,16,128]{2,1,0:T(8,128)(2,1)S(1)}, u32[]{:S(2)}, u32[]{:S(2)}) collective-permute-start(bf16[64,16,128]{2,1,0:T(8,128)(2,1)S(1)} %get-tuple-element.30), channel_id=1, source_target_pairs={{0,1},{1,0},{2,3},{3,2},{4,5},{5,4},{6,7},{7,6},{8,9},{9,8},{10,11... | collective-permute-start | bytes 786440 | tf_op jit(solution)/shard_map/ppermute | solution.py:301
  51.4 15.4 %collective-permute-start.21 = (bf16[64,16,128]{2,1,0:T(8,128)(2,1)S(1)}, bf16[64,16,128]{2,1,0:T(8,128)(2,1)S(1)}, u32[]{:S(2)}, u32[]{:S(2)}) collective-permute-start(bf16[64,16,128]{2,1,0:T(8,128)(2,1)S(1)} %add_convert_fusion.refs_0_), channel_id=1, source_target_pairs={{0,4},{4,0},{8,12},{12,8},{1,5},{5,1},{9,13},{13,9},{2,6},{6,2},{1... | collective-permute-start | bytes 786440 | tf_op jit(solution)/shard_map/ppermute | solution.py:304
  51.8 16.2 %collective-permute-start.22 = (bf16[64,16,128]{2,1,0:T(8,128)(2,1)S(1)}, bf16[64,16,128]{2,1,0:T(8,128)(2,1)S(1)}, u32[]{:S(2)}, u32[]{:S(2)}) collective-permute-start(bf16[64,16,128]{2,1,0:T(8,128)(2,1)S(1)} %add_convert_fusion.refs_0_), channel_id=1, source_target_pairs={{0,8},{4,12},{8,0},{12,4},{1,9},{5,13},{9,1},{13,5},{2,10},{6,14},... | collective-permute-start | bytes 786440 | tf_op jit(solution)/shard_map/ppermute | solution.py:304
  53.2 14.8 %collective-permute-start.23 = (bf16[64,16,128]{2,1,0:T(8,128)(2,1)S(1)}, bf16[64,16,128]{2,1,0:T(8,128)(2,1)S(1)}, u32[]{:S(2)}, u32[]{:S(2)}) collective-permute-start(bf16[64,16,128]{2,1,0:T(8,128)(2,1)S(1)} %add_convert_fusion.refs_0_), channel_id=1, source_target_pairs={{0,12},{4,8},{8,4},{12,0},{1,13},{5,9},{9,5},{13,1},{2,14},{6,10},... | collective-permute-start | bytes 786440 | tf_op jit(solution)/shard_map/ppermute | solution.py:304
  63.5 12.9 %collective-permute-start.8 = (bf16[64,16,128]{2,1,0:T(8,128)(2,1)S(1)}, bf16[64,16,128]{2,1,0:T(8,128)(2,1)S(1)}, u32[]{:S(2)}, u32[]{:S(2)}) collective-permute-start(bf16[64,16,128]{2,1,0:T(8,128)(2,1)S(1)} %add_convert_fusion.1.refs_0_), channel_id=1, source_target_pairs={{0,1},{1,0},{2,3},{3,2},{4,5},{5,4},{6,7},{7,6},{8,9},{9,8},{10,11... | collective-permute-start | bytes 786440 | tf_op jit(solution)/shard_map/ppermute | solution.py:304
  63.6 21.6 %collective-permute-start.9 = (bf16[64,16,128]{2,1,0:T(8,128)(2,1)S(1)}, bf16[64,16,128]{2,1,0:T(8,128)(2,1)S(1)}, u32[]{:S(2)}, u32[]{:S(2)}) collective-permute-start(bf16[64,16,128]{2,1,0:T(8,128)(2,1)S(1)} %add_convert_fusion.1.refs_0_), channel_id=1, source_target_pairs={{0,2},{1,3},{2,0},{3,1},{4,6},{5,7},{6,4},{7,5},{8,10},{9,11},{10,... | collective-permute-start | bytes 786440 | tf_op jit(solution)/shard_map/ppermute | solution.py:304
  66.8 18.4 %collective-permute-start.10 = (bf16[64,16,128]{2,1,0:T(8,128)(2,1)S(1)}, bf16[64,16,128]{2,1,0:T(8,128)(2,1)S(1)}, u32[]{:S(2)}, u32[]{:S(2)}) collective-permute-start(bf16[64,16,128]{2,1,0:T(8,128)(2,1)S(1)} %add_convert_fusion.1.refs_0_), channel_id=1, source_target_pairs={{0,3},{1,2},{2,1},{3,0},{4,7},{5,6},{6,5},{7,4},{8,11},{9,10},{10,... | collective-permute-start | bytes 786440 | tf_op jit(solution)/shard_map/ppermute | solution.py:304
  75.5 16.4 %collective-permute-start.24 = (bf16[64,16,128]{2,1,0:T(8,128)(2,1)S(1)}, bf16[64,16,128]{2,1,0:T(8,128)(2,1)S(1)}, u32[]{:S(2)}, u32[]{:S(2)}) collective-permute-start(bf16[64,16,128]{2,1,0:T(8,128)(2,1)S(1)} %get-tuple-element.46), channel_id=1, source_target_pairs={{0,4},{4,0},{8,12},{12,8},{1,5},{5,1},{9,13},{13,9},{2,6},{6,2},{1... | collective-permute-start | bytes 786440 | tf_op jit(solution)/shard_map/ppermute | solution.py:301
  75.8 18.6 %collective-permute-start.25 = (bf16[64,16,128]{2,1,0:T(8,128)(2,1)S(1)}, bf16[64,16,128]{2,1,0:T(8,128)(2,1)S(1)}, u32[]{:S(2)}, u32[]{:S(2)}) collective-permute-start(bf16[64,16,128]{2,1,0:T(8,128)(2,1)S(1)} %get-tuple-element.47), channel_id=1, source_target_pairs={{0,8},{4,12},{8,0},{12,4},{1,9},{5,13},{9,1},{13,5},{2,10},{6,14},... | collective-permute-start | bytes 786440 | tf_op jit(solution)/shard_map/ppermute | solution.py:301
  76.4 18.0 %collective-permute-start.26 = (bf16[64,16,128]{2,1,0:T(8,128)(2,1)S(1)}, bf16[64,16,128]{2,1,0:T(8,128)(2,1)S(1)}, u32[]{:S(2)}, u32[]{:S(2)}) collective-permute-start(bf16[64,16,128]{2,1,0:T(8,128)(2,1)S(1)} %get-tuple-element.48), channel_id=1, source_target_pairs={{0,12},{4,8},{8,4},{12,0},{1,13},{5,9},{9,5},{13,1},{2,14},{6,10},... | collective-permute-start | bytes 786440 | tf_op jit(solution)/shard_map/ppermute | solution.py:301
  90.9 8.3 %collective-permute-start.11 = (bf16[64,16,128]{2,1,0:T(8,128)(2,1)S(1)}, bf16[64,16,128]{2,1,0:T(8,128)(2,1)S(1)}, u32[]{:S(2)}, u32[]{:S(2)}) collective-permute-start(bf16[64,16,128]{2,1,0:T(8,128)(2,1)S(1)} %get-tuple-element.34), channel_id=1, source_target_pairs={{0,4},{4,0},{8,12},{12,8},{1,5},{5,1},{9,13},{13,9},{2,6},{6,2},{1... | collective-permute-start | bytes 786440 | tf_op jit(solution)/shard_map/ppermute | solution.py:301
  91.2 9.3 %collective-permute-start.12 = (bf16[64,16,128]{2,1,0:T(8,128)(2,1)S(1)}, bf16[64,16,128]{2,1,0:T(8,128)(2,1)S(1)}, u32[]{:S(2)}, u32[]{:S(2)}) collective-permute-start(bf16[64,16,128]{2,1,0:T(8,128)(2,1)S(1)} %get-tuple-element.35), channel_id=1, source_target_pairs={{0,8},{4,12},{8,0},{12,4},{1,9},{5,13},{9,1},{13,5},{2,10},{6,14},... | collective-permute-start | bytes 786440 | tf_op jit(solution)/shard_map/ppermute | solution.py:301
  91.9 8.6 %collective-permute-start.13 = (bf16[64,16,128]{2,1,0:T(8,128)(2,1)S(1)}, bf16[64,16,128]{2,1,0:T(8,128)(2,1)S(1)}, u32[]{:S(2)}, u32[]{:S(2)}) collective-permute-start(bf16[64,16,128]{2,1,0:T(8,128)(2,1)S(1)} %get-tuple-element.36), channel_id=1, source_target_pairs={{0,12},{4,8},{8,4},{12,0},{1,13},{5,9},{9,5},{13,1},{2,14},{6,10},... | collective-permute-start | bytes 786440 | tf_op jit(solution)/shard_map/ppermute | solution.py:301
  94.6 10.2 %collective-permute-start.27 = (bf16[64,16,128]{2,1,0:T(8,128)(2,1)S(1)}, bf16[64,16,128]{2,1,0:T(8,128)(2,1)S(1)}, u32[]{:S(2)}, u32[]{:S(2)}) collective-permute-start(bf16[64,16,128]{2,1,0:T(8,128)(2,1)S(1)} %get-tuple-element.50), channel_id=1, source_target_pairs={{0,1},{1,0},{2,3},{3,2},{4,5},{5,4},{6,7},{7,6},{8,9},{9,8},{10,11... | collective-permute-start | bytes 786440 | tf_op jit(solution)/shard_map/ppermute | solution.py:301
  98.1 19.5 %collective-permute-start.28 = (bf16[64,16,128]{2,1,0:T(8,128)(2,1)S(1)}, bf16[64,16,128]{2,1,0:T(8,128)(2,1)S(1)}, u32[]{:S(2)}, u32[]{:S(2)}) collective-permute-start(bf16[64,16,128]{2,1,0:T(8,128)(2,1)S(1)} %get-tuple-element.51), channel_id=1, source_target_pairs={{0,2},{1,3},{2,0},{3,1},{4,6},{5,7},{6,4},{7,5},{8,10},{9,11},{10,... | collective-permute-start | bytes 786440 | tf_op jit(solution)/shard_map/ppermute | solution.py:301
  99.1 18.4 %collective-permute-start.29 = (bf16[64,16,128]{2,1,0:T(8,128)(2,1)S(1)}, bf16[64,16,128]{2,1,0:T(8,128)(2,1)S(1)}, u32[]{:S(2)}, u32[]{:S(2)}) collective-permute-start(bf16[64,16,128]{2,1,0:T(8,128)(2,1)S(1)} %get-tuple-element.52), channel_id=1, source_target_pairs={{0,3},{1,2},{2,1},{3,0},{4,7},{5,6},{6,5},{7,4},{8,11},{9,10},{10,... | collective-permute-start | bytes 786440 | tf_op jit(solution)/shard_map/ppermute | solution.py:301
